TPU v7x, 32 devices: a whole 2x2x4 slice. The times are simulated.
32 devices in a mesh: seq: 16 (over z, y, x), tp: 2 (over core).
Axes of the slice: x: 2, y: 2, z: 4, core: 2. Of those that a mesh axis runs over, the one named last changes fastest.
Arguments:
- img: bfloat16 [4, 512, 3072], P(None, 'seq', 'tp'), may hold values from -6 to 6
- txt: bfloat16 [4, 64, 3072], P(None, 'seq', 'tp'), may hold values from -6 to 6
- prev_mod: bfloat16 [4, 512, 3072], P(None, 'seq', 'tp'), may hold values from -47 to 47
- cache: float32 [4, 512, 3072], P(None, 'seq', 'tp'), may hold values from -6 to 6
- modulation: bfloat16 [3, 4, 3072], P(None, None, 'tp'), may hold values from -4 to 4
- w_qkv: bfloat16 [3072, 3, 2048], P('seq', None, 'tp'), may hold values from -1 to 1, as said below
- qk_gain: float32 [2, 2048], P(None, 'tp'), may hold values from 0.5 to 6, as said below
- output_weight: bfloat16 [2048, 3072], P('tp'), may hold values from -0.1875 to 0.1875
- text_len: int32 [4], replicated, may hold values from 1 to 64
- refresh: int32 [4], replicated, may hold values from 0 to 1, as said below
Outputs:
- out_img: float32 [4, 512, 3072], P(None, 'seq', 'tp')
- new_cache: float32 [4, 512, 3072], P(None, 'seq', 'tp')
- rel_l1: float32 [4], replicated
Inputs may be any that keep to these rules, and one draw needn't show every extreme that they name: `refresh`: at least one sequence has flag 1 and at least one has flag 0. `w_qkv`: entries of spread about one over the square root of 3072. `qk_gain`: positive.
All inputs are finite; a program needn't handle non-finite values.
Results may differ from a plain program's by a relative error of at most 0.013.
The roundings to bfloat16 on the way count: a program that leaves them out, or rounds other values in their place, can miss the bound.
Values may be sent and summed in bfloat16 or wider, within the bound.
A program may use at most 128 MiB of HBM per device.

v0:
```python
import jax
import jax.numpy as jnp
from jax import lax
from jax.sharding import PartitionSpec as P

HD = 128
EPS = 0.1
NEG = -1e30


def unit_heads(block, gain):
    shaped = block.reshape(block.shape[:-1] + (block.shape[-1] // HD, HD))
    scaled = shaped * lax.rsqrt(jnp.mean(jnp.square(shaped), axis=-1, keepdims=True) + EPS)
    return scaled.reshape(block.shape) * gain


def local(img, txt, prev_mod, cache, modulation, w_qkv, qk_gain, output_weight, text_len, refresh):
    batch, img_rows, width_loc = img.shape
    txt_rows = txt.shape[1]
    rows = txt_rows + img_rows
    joined = jnp.concatenate([txt, img], axis=1)
    local_mods = modulation.astype(jnp.float32)
    wide, wide_mod = (
        lax.all_gather(joined, "tp", axis=2, tiled=True),
        lax.all_gather(modulation, "tp", axis=2, tiled=True),
    )
    wide_mods = wide_mod.astype(jnp.float32)
    values = wide.astype(jnp.float32)
    center = jnp.mean(values, axis=2, keepdims=True)
    spread = jnp.mean(jnp.square(values - center), axis=2, keepdims=True)
    normed = (values - center) * lax.rsqrt(spread + EPS)
    modded = (normed * (1.0 + wide_mods[1][:, None, :]) + wide_mods[0][:, None, :]).astype(
        jnp.bfloat16
    )
    offset = lax.axis_index("tp") * width_loc
    own_image = lax.dynamic_slice_in_dim(modded[:, txt_rows:, :], offset, width_loc, 2)
    previous = prev_mod.astype(jnp.float32)
    gap = jnp.sum(jnp.abs(own_image.astype(jnp.float32) - previous), axis=(1, 2))
    base_sum = jnp.sum(jnp.abs(previous), axis=(1, 2))
    numer, denom = lax.psum((gap, base_sum), ("seq", "tp"))
    rel_l1 = numer / jnp.maximum(denom, 1.0)
    columns = w_qkv.shape[2]
    projected = jnp.einsum(
        "btd,dkc->btkc",
        modded,
        lax.all_gather(w_qkv, "seq", axis=0, tiled=True),
        preferred_element_type=jnp.float32,
    )
    heads = columns // HD
    query = unit_heads(projected[:, txt_rows:, 0, :], qk_gain[0]).astype(jnp.bfloat16)
    query_heads = query.reshape(batch, img_rows, heads, HD)
    keyed = unit_heads(projected[:, :, 1, :], qk_gain[1]).astype(jnp.bfloat16)
    valued = projected[:, :, 2, :].astype(jnp.bfloat16)
    paired = jnp.stack([keyed, valued], axis=2)
    score_scale = 1.0 / HD**0.5
    start_top = jnp.full((batch, heads, img_rows), NEG, jnp.float32)
    piece = lax.all_gather(paired, "seq", axis=1, tiled=True)
    top = start_top
    count = piece.shape[1]
    index = jnp.arange(count, dtype=jnp.int32)
    slot = index % rows
    text_pos = index // rows * txt_rows + slot
    valid = (slot >= txt_rows)[None, :] | (text_pos[None, :] < text_len[:, None])
    keys = piece[:, :, 0, :].reshape(batch, count, heads, HD)
    vals = piece[:, :, 1, :].reshape(batch, count, heads, HD)
    logit_scores = (
        jnp.einsum("bqhc,bkhc->bhqk", query_heads, keys, preferred_element_type=jnp.float32)
        * score_scale
    )
    logit_scores = jnp.where(valid[:, None, None, :], logit_scores, NEG)
    new_top = jnp.maximum(top, jnp.max(logit_scores, axis=3))
    attention_weights = jnp.where(
        valid[:, None, None, :], jnp.exp(logit_scores - new_top[..., None]), 0.0
    )
    total = jnp.sum(attention_weights, axis=3)
    summed_output = jnp.einsum(
        "bhqk,bkhc->bhqc",
        attention_weights.astype(jnp.bfloat16),
        vals,
        preferred_element_type=jnp.float32,
    )
    top, total, summed_output = (new_top, total, summed_output)
    attended_values = (summed_output / total[..., None]).astype(jnp.bfloat16)
    attended_values = attended_values.transpose(0, 2, 1, 3).reshape(batch, img_rows, columns)
    partial_output = jnp.einsum(
        "pxr,ro->pxo", attended_values, output_weight, preferred_element_type=jnp.float32
    )
    whole = lax.psum(partial_output.astype(jnp.bfloat16), "tp").astype(jnp.float32)
    mixed_heads = lax.dynamic_slice_in_dim(whole, lax.axis_index("tp") * width_loc, width_loc, 2)
    resid = local_mods[2][:, None, :] * mixed_heads
    flag = (refresh == 1)[:, None, None]
    new_cache = jnp.where(flag, resid, cache)
    out_img = img.astype(jnp.float32) + new_cache
    return (out_img, new_cache, rel_l1)


def solution(mesh):
    return jax.shard_map(
        local,
        mesh=mesh,
        in_specs=(
            P(None, "seq", "tp"),
            P(None, "seq", "tp"),
            P(None, "seq", "tp"),
            P(None, "seq", "tp"),
            P(None, None, "tp"),
            P("seq", None, "tp"),
            P(None, "tp"),
            P("tp", None),
            P(),
            P(),
        ),
        out_specs=(P(None, "seq", "tp"), P(None, "seq", "tp"), P()),
        check_vma=False,
    )
```

profile of v0, /device:TPU:0, one launch (start us, length us, event | category | flops | bytes accessed | tf_op | source)
XLA Modules:
  0.0 434.7 jit_solution(10169232465015273428)
XLA Ops:
  8.0 2.2 all_gather.13
  10.2 1.1 pad_maximum_fusion.1
  11.3 2.5 all_gather.12
  15.0 209.3 %all-gather.3.cloned.1.call-done = bf16[3072,3,1024]{2,0,1:T(8,128)(2,1)} async-done(((bf16[192,3,1024]{2,0,1:T(8,128)(2,1)}), bf16[3072,3,1024]{2,0,1:T(8,128)(2,1)}) %all-gather.3.cloned.1.call-update) | async-done | bytes 18874384 | tf_op jit(solution)/shard_map/all_gather | solution.py:46
  224.3 8.1 %fusion = f32[4,36,3,1024]{3,1,2,0:T(8,128)S(1)} fusion(bf16[3072,3,1024]{2,0,1:T(8,128)(2,1)} %all-gather.3.cloned.1.call-done, bf16[4,36,3072]{2,1,0:T(8,128)(2,1)S(1)} %fusion.17), kind=kOutput, calls=%fused_computation | convolution fusion | flops 2717908992 | bytes 21528576 | tf_op jit(solution)/shard_map/btd,dkc->btkc/dot_general | solution.py:43
  232.4 0.9 slice_multiply_fusion
  234.1 1.2 reshape.130
  236.1 1.0 copy.47
  237.2 1.0 mul.103
  238.3 1.3 mul.104
  239.9 1.1 pad_maximum_fusion
  241.0 1.3 copy.50
  242.4 1.1 slice.53
  243.5 1.3 fusion.49
  244.8 40.5 %all-reduce = (f32[4]{0:T(128)S(1)}, f32[4]{0:T(128)S(1)}) all-reduce(f32[4]{0:T(128)S(1)} %get-tuple-element.4, f32[4]{0:T(128)S(1)} %get-tuple-element.3), channel_id=1, replica_groups=mesh['seq'=16,'tp'=2] {'seq','tp'}, use_global_device_ids=true, to_apply=%region_8.9 | all-reduce | flops 8 | bytes 64 | tf_op jit(solution)/shard_map/psum | solution.py:40
  286.0 77.3 %all-gather.5.cloned.1.call-done = bf16[4,576,2,1024]{3,0,2,1:T(4,128)(2,1)} async-done(((bf16[4,36,2,1024]{3,0,2,1:T(4,128)(2,1)}), bf16[4,576,2,1024]{3,0,2,1:T(4,128)(2,1)}) %all-gather.5.cloned.1.call-update) | async-done | bytes 9437200 | tf_op jit(solution)/shard_map/all_gather | solution.py:57
  363.3 10.7 %fusion.70 = (bf16[4,576,1,1024]{3,0,2,1:T(4,128)(2,1)}, bf16[4,576,1,1024]{3,0,2,1:T(4,128)(2,1)}) fusion(bf16[4,576,2,1024]{3,0,2,1:T(4,128)(2,1)} %all-gather.5.cloned.1.call-done), kind=kLoop, calls=%fused_computation.82 | loop fusion | bytes 18874368 | tf_op jit(solution)/shard_map/slice | solution.py:64
  374.0 8.0 %reshape.131 = bf16[4,576,8,128]{3,2,0,1:T(8,128)(2,1)} reshape(bf16[4,576,1,1024]{3,0,2,1:T(4,128)(2,1)} %get-tuple-element.9) | data formatting | bytes 9437184 | tf_op jit(solution)/shard_map/reshape;squeeze | solution.py:64
  382.0 7.5 %fusion.13 = (f32[4,8,32]{2,1,0:T(8,128)S(1)}, f32[4,8,32,576]{3,2,1,0:T(8,128)S(1)}) fusion(pred[4,576]{1,0:T(4,128)(4,1)S(1)} %compare_or_fusion, bf16[4,576,8,128]{3,2,0,1:T(8,128)(2,1)} %reshape.131, bf16[4,32,8,128]{3,2,1,0:T(8,128)(2,1)S(1)} %fusion.54), kind=kOutput, calls=%fused_computation.15 | convolution fusion | flops 152763392 | bytes 7346432 | tf_op jit(solution)/shard_map/bqhc,bkhc->bhqk/dot_general | solution.py:67
  389.5 8.0 %reshape.132 = bf16[4,576,8,128]{3,2,0,1:T(8,128)(2,1)} reshape(bf16[4,576,1,1024]{3,0,2,1:T(4,128)(2,1)} %get-tuple-element.10) | data formatting | bytes 9437184 | tf_op jit(solution)/shard_map/reshape;squeeze | solution.py:65
  398.4 8.1 %fusion.41 = bf16[4,8,4,8,128]{4,3,2,1,0:T(8,128)(2,1)S(1)} fusion(bf16[4,576,8,128]{3,2,0,1:T(8,128)(2,1)} %reshape.132, f32[4,8,32,576]{3,2,1,0:T(8,128)S(1)} %get-tuple-element.16, f32[4,8,32]{2,1,0:T(8,128)S(1)} %broadcast_maximum_fusion, pred[4,576]{1,0:T(4,128)(4,1)S(1)} %compare_or_fusion, f32[4,32,8]{1,2,0:T(8,128)S(1)} %bitcast.67), kind=kOutput, calls=%fused_computation.30 | convolution fusion | flops 154206208 | bytes 7350528 | tf_op jit(solution)/shard_map/bhqk,bkhc->bhqc/dot_general | solution.py:76
  406.6 1.9 fusion.8
  409.7 16.1 %all-reduce.3.cloned.1.call-done = bf16[4,32,3072]{2,1,0:T(8,128)(2,1)} async-done(((bf16[4,32,3072]{2,1,0:T(8,128)(2,1)}), bf16[4,32,3072]{2,1,0:T(8,128)(2,1)}) %all-reduce.3.cloned.1.call-update) | async-done | bytes 786448 | tf_op jit(solution)/shard_map/psum | solution.py:88
  425.8 2.4 convert_add_fusion
  (49 shorter events, 6.9 us)
Async XLA Ops:
  7.2 217.1 %all-gather.3.cloned.1.call-start = ((), (), s32[]{:S(2)}) async-start(), calls=%async_computation | async-start | bytes 20054016 | tf_op jit(solution)/shard_map/all_gather | solution.py:46
  7.9 6.6 %copy-start.3 = (f32[2,1024]{1,0:T(2,128)S(1)}, f32[2,1024]{1,0:T(2,128)}, u32[]{:S(2)}) copy-start(f32[2,1024]{1,0:T(2,128)} %param.16) | copy-start | bytes 24580
  7.9 355.4 %all-gather.5.cloned.1.call-start = ((), (), s32[]{:S(2)}) async-start(), calls=%async_computation.1 | async-start | bytes 10027008 | tf_op jit(solution)/shard_map/all_gather | solution.py:57
  239.9 3.6 copy-start.2
  239.9 45.4 %copy-start.4 = (s32[4]{0:T(128)S(1)}, s32[4]{0:T(128)}, u32[]{:S(2)}) copy-start(s32[4]{0:T(128)} %param.18) | copy-start | bytes 52
  242.3 183.5 %all-reduce.3.cloned.1.call-start = ((), (), s32[]{:S(2)}) async-start(), calls=%async_computation.2 | async-start | bytes 1572864 | tf_op jit(solution)/shard_map/psum | solution.py:88
  397.6 8.9 %slice-start = ((s8[6291456]{0:T(1024)(128)(4,1)}), s8[4194304]{0:T(1024)(128)(4,1)S(1)}, s32[]{:S(2)}) async-start(s8[6291456]{0:T(1024)(128)(4,1)} %bitcast.62), calls=%async_computation.3 | async-start | bytes 8388608
  398.4 8.1 %slice-start.1 = ((s8[6291456]{0:T(1024)(128)(4,1)}), s8[2097152]{0:T(1024)(128)(4,1)S(1)}, s32[]{:S(2)}) async-start(s8[6291456]{0:T(1024)(128)(4,1)} %bitcast.62), calls=%async_computation.4 | async-start | bytes 4194304
  406.5 1.9 copy-start.5
  406.5 19.2 %copy-start = (bf16[4,32,1536]{2,1,0:T(8,128)(2,1)S(1)}, bf16[4,32,1536]{2,1,0:T(8,128)(2,1)}, u32[]{:S(2)}) copy-start(bf16[4,32,1536]{2,1,0:T(8,128)(2,1)} %param.10) | copy-start | bytes 1179652
  406.6 19.2 %copy-start.1 = (f32[4,32,1536]{2,1,0:T(8,128)S(1)}, f32[4,32,1536]{2,1,0:T(8,128)}, u32[]{:S(2)}) copy-start(f32[4,32,1536]{2,1,0:T(8,128)} %param.13) | copy-start | bytes 2359300
Sparse Core Ops, SparseCore 0:
  10.6 213.6 all-gather.2
  242.4 120.8 all-gather.4
  408.6 17.1 all-reduce.2
where the time goes:
time: 436 us; the launch traced here: 435 us
  waiting for transfers between devices  303 us (69%)
  blocking collectives  45.3 us (10%)
  local copies, waits for them, and re-layouts  34.7 us (8%)
  matrix products  25.6 us (6%)
  between operations  14 us (3%)
  other arithmetic  11.8 us (3%)
    all_gather x1, waiting for transfers between devices, local(): lax.all_gather(w_qkv, 'seq', axis=0, tiled=True)  209 us
    all_gather x1, waiting for transfers between devices, local(): piece = lax.all_gather(paired, 'seq', axis=1, tiled=True)  77.3 us
    psum x1, blocking collectives, local(): numer, denom = lax.psum((gap, base_sum), ('seq', 'tp'))  40.5 us
    psum x1, waiting for transfers between devices, local(): lax.psum(partial_output.astype(jnp.bfloat16), 'tp').astype(jnp.float32)  16.1 us
    slice x1, local copies, waits for them, and re-layouts, local(): keys = piece[:, :, 0, :].reshape(batch, count, heads, HD)  10.7 us
  transfers between devices with their start and end apart: 3, of which 3 were waited for; matrix products, arithmetic and copies ran while one was open for 2% of the time, Pallas kernels for 0%

commit v1 on v0

--- a/solution.py
+++ b/solution.py
@@ -6,6 +6,13 @@
 HD = 128
 EPS = 0.1
 NEG = -1e30
+
+
+def all_by_exchange(x, name, dim):
+    n_dev = lax.axis_size(name)
+    pieces = jnp.stack([x for _ in range(n_dev)])
+    pieces = lax.all_to_all(pieces, name, split_axis=0, concat_axis=0)
+    return jnp.concatenate(pieces, axis=dim)
 
 
 def unit_heads(block, gain):
@@ -43,7 +50,7 @@
     projected = jnp.einsum(
         "btd,dkc->btkc",
         modded,
-        lax.all_gather(w_qkv, "seq", axis=0, tiled=True),
+        all_by_exchange(w_qkv, "seq", 0),
         preferred_element_type=jnp.float32,
     )
     heads = columns // HD

time: 436 us -> 671 us (1.54)
  waiting for transfers between devices: 303 us -> 445 us
  blocking collectives: 45.3 us -> 121 us
  local copies, waits for them, and re-layouts: 34.7 us -> 51.9 us
  starting transfers between devices: 0.12 us -> 8.61 us
  matrix products: 25.6 us -> 18.6 us
    all_to_all x0 -> x1, waiting for transfers between devices: none -> 349 us  [all_by_exchange(): pieces = lax.all_to_all(pieces, name, split_axis=0, concat_axis=0)]
    all_gather x1 -> x0, waiting for transfers between devices: 209 us -> none  [local(): lax.all_gather(w_qkv, 'seq', axis=0, tiled=True)]
    psum x1, blocking collectives: 40.5 us -> 117 us  [local(): numer, denom = lax.psum((gap, base_sum), ('seq', 'tp'))]
    all_to_all x0 -> x1, local copies, waits for them, and re-layouts: none -> 9.54 us  [all_by_exchange(): pieces = lax.all_to_all(pieces, name, split_axis=0, concat_axis=0)]
    all_to_all x0 -> x1, starting transfers between devices: none -> 8.53 us  [all_by_exchange(): pieces = lax.all_to_all(pieces, name, split_axis=0, concat_axis=0)]
    another operation x0 -> x1, local copies, waits for them, and re-layouts: none -> 7.56 us  [all_by_exchange(): pieces = jnp.stack([x for _ in range(n_dev)])]
  transfers between devices with their start and end apart: 3 -> 3, of which waited for: 3 -> 3; matrix products, arithmetic and copies ran while one was open for 2% -> 1% of each run, Pallas kernels for 0% -> 0%
where the time goes in v1:
time: 671 us; the launch traced here: 670 us
  waiting for transfers between devices  445 us (66%)
  blocking collectives  121 us (18%)
  local copies, waits for them, and re-layouts  51.9 us (8%)
  matrix products  18.6 us (3%)
  between operations  14.4 us (2%)
  other arithmetic  10.8 us (2%)
  starting transfers between devices  8.61 us (1%)
    all_to_all x1, waiting for transfers between devices, all_by_exchange(): pieces = lax.all_to_all(pieces, name, split_axis=0, concat_axis=0)  349 us
    psum x1, blocking collectives, local(): numer, denom = lax.psum((gap, base_sum), ('seq', 'tp'))  117 us
    all_gather x1, waiting for transfers between devices, local(): piece = lax.all_gather(paired, 'seq', axis=1, tiled=True)  79.9 us
    psum x1, waiting for transfers between devices, local(): lax.psum(partial_output.astype(jnp.bfloat16), 'tp').astype(jnp.float32)  16.1 us
  transfers between devices with their start and end apart: 3, of which 3 were waited for; matrix products, arithmetic and copies ran while one was open for 1% of the time, Pallas kernels for 0%

profile of v1, /device:TPU:0, one launch (start us, length us, event | category | flops | bytes accessed | tf_op | source)
XLA Modules:
  0.0 670.3 jit_solution(8741818420026604432)
XLA Ops:
  7.2 7.6 %stack.4 = bf16[16,192,3,1024]{3,1,2,0:T(8,128)(2,1)} broadcast(bf16[192,3,1024]{2,0,1:T(8,128)(2,1)} %param.15), dimensions={1,2,3} | broadcast | bytes 20054016 | tf_op jit(solution)/shard_map/stack | solution.py:13
  14.7 8.5 %all-to-all-start = ((bf16[16,192,3,1024]{3,1,2,0:T(8,128)(2,1)}), bf16[16,192,3,1024]{3,1,2,0:T(8,128)(2,1)}, u32[]{:S(2)}, u32[]{:S(2)}) async-start(bf16[16,192,3,1024]{3,1,2,0:T(8,128)(2,1)} %stack.4), calls=%async_computation | async-start | bytes 37748736 | tf_op jit(solution)/shard_map/all_to_all | solution.py:14
  23.3 1.9 all_gather.10
  25.4 2.5 all_gather.9
  29.1 348.7 %all-to-all-done = bf16[16,192,3,1024]{3,1,2,0:T(8,128)(2,1)} async-done(((bf16[16,192,3,1024]{3,1,2,0:T(8,128)(2,1)}), bf16[16,192,3,1024]{3,1,2,0:T(8,128)(2,1)}, u32[]{:S(2)}, u32[]{:S(2)}) %all-to-all-start) | async-done | bytes 18874400 | tf_op jit(solution)/shard_map/all_to_all | solution.py:14
  377.7 9.5 %copy.49 = bf16[16,192,3,1024]{3,1,0,2:T(8,128)(2,1)S(1)} copy(bf16[16,192,3,1024]{3,1,2,0:T(8,128)(2,1)} %all-to-all-done) | data formatting | bytes 37748736 | tf_op jit(solution)/shard_map/all_to_all | solution.py:14
  387.3 3.4 fusion.44
  392.4 1.2 reshape.136
  395.5 1.0 mul.103
  396.6 1.3 mul.104
  398.2 1.1 pad_maximum_fusion
  399.3 1.3 copy.54
  400.7 1.1 slice.53
  401.8 1.3 fusion.48
  403.1 117.1 %all-reduce = (f32[4]{0:T(128)S(1)}, f32[4]{0:T(128)S(1)}) all-reduce(f32[4]{0:T(128)S(1)} %get-tuple-element.4, f32[4]{0:T(128)S(1)} %get-tuple-element.3), channel_id=1, replica_groups=mesh['seq'=16,'tp'=2] {'seq','tp'}, use_global_device_ids=true, to_apply=%region_8.9 | all-reduce | flops 8 | bytes 64 | tf_op jit(solution)/shard_map/psum | solution.py:47
  520.9 79.9 %all-gather.2.cloned.1.call-done = bf16[4,576,2,1024]{3,0,2,1:T(4,128)(2,1)} async-done(((bf16[4,36,2,1024]{3,0,2,1:T(4,128)(2,1)}), bf16[4,576,2,1024]{3,0,2,1:T(4,128)(2,1)}) %all-gather.2.cloned.1.call-update) | async-done | bytes 9437200 | tf_op jit(solution)/shard_map/all_gather | solution.py:64
  600.7 10.7 %fusion.69 = (bf16[4,576,1,1024]{3,0,2,1:T(4,128)(2,1)}, bf16[4,576,1,1024]{3,0,2,1:T(4,128)(2,1)}) fusion(bf16[4,576,2,1024]{3,0,2,1:T(4,128)(2,1)} %all-gather.2.cloned.1.call-done), kind=kLoop, calls=%fused_computation.81 | loop fusion | bytes 18874368 | tf_op jit(solution)/shard_map/slice | solution.py:71
  611.4 8.0 %reshape.138 = bf16[4,576,8,128]{3,2,0,1:T(8,128)(2,1)} reshape(bf16[4,576,1,1024]{3,0,2,1:T(4,128)(2,1)} %get-tuple-element.10) | data formatting | bytes 9437184 | tf_op jit(solution)/shard_map/reshape;squeeze | solution.py:72
  619.4 8.2 %reshape.137 = bf16[4,576,8,128]{3,2,0,1:T(8,128)(2,1)} reshape(bf16[4,576,1,1024]{3,0,2,1:T(4,128)(2,1)} %get-tuple-element.9) | data formatting | bytes 9437184 | tf_op jit(solution)/shard_map/reshape;squeeze | solution.py:71
  627.6 7.7 %fusion.11 = (f32[4,8,32]{2,1,0:T(8,128)S(1)}, f32[4,8,32,576]{3,2,1,0:T(8,128)S(1)}) fusion(pred[4,576]{1,0:T(4,128)(4,1)S(1)} %compare_or_fusion, bf16[4,576,8,128]{3,2,0,1:T(8,128)(2,1)} %reshape.137, bf16[4,32,8,128]{3,2,1,0:T(8,128)(2,1)S(1)} %fusion.53), kind=kOutput, calls=%fused_computation.13 | convolution fusion | flops 152763392 | bytes 7346432 | tf_op jit(solution)/shard_map/bqhc,bkhc->bhqk/dot_general | solution.py:74
  636.1 5.6 fusion.39
  641.8 1.9 fusion.6
  645.0 16.1 %all-reduce.3.cloned.1.call-done = bf16[4,32,3072]{2,1,0:T(8,128)(2,1)} async-done(((bf16[4,32,3072]{2,1,0:T(8,128)(2,1)}), bf16[4,32,3072]{2,1,0:T(8,128)(2,1)}) %all-reduce.3.cloned.1.call-update) | async-done | bytes 786448 | tf_op jit(solution)/shard_map/psum | solution.py:95
  661.0 2.4 convert_add_fusion
  (61 shorter events, 8.2 us)
Async XLA Ops:
  14.7 8.6 %copy-start.4 = (bf16[3,4,1536]{2,1,0:T(4,128)(2,1)S(1)}, bf16[3,4,1536]{2,1,0:T(4,128)(2,1)}, u32[]{:S(2)}) copy-start(bf16[3,4,1536]{2,1,0:T(4,128)(2,1)} %param.14) | copy-start | bytes 110596
  14.7 10.5 %copy-start = (bf16[4,32,1536]{2,1,0:T(8,128)(2,1)S(1)}, bf16[4,32,1536]{2,1,0:T(8,128)(2,1)}, u32[]{:S(2)}) copy-start(bf16[4,32,1536]{2,1,0:T(8,128)(2,1)} %param.10) | copy-start | bytes 1179652
  14.7 10.5 %copy-start.5 = (bf16[4,4,1536]{2,1,0:T(4,128)(2,1)S(1)}, bf16[4,4,1536]{2,1,0:T(4,128)(2,1)}, u32[]{:S(2)}) copy-start(bf16[4,4,1536]{2,1,0:T(4,128)(2,1)} %param.11) | copy-start | bytes 147460
  14.7 363.0 %all-to-all-start = ((bf16[16,192,3,1024]{3,1,2,0:T(8,128)(2,1)}), bf16[16,192,3,1024]{3,1,2,0:T(8,128)(2,1)}, u32[]{:S(2)}, u32[]{:S(2)}) async-start(bf16[16,192,3,1024]{3,1,2,0:T(8,128)(2,1)} %stack.4), calls=%async_computation | async-start | bytes 37748736 | tf_op jit(solution)/shard_map/all_to_all | solution.py:14
  23.3 5.3 copy-start.6
  23.3 577.4 %all-gather.2.cloned.1.call-start = ((), (), s32[]{:S(2)}) async-start(), calls=%async_computation.1 | async-start | bytes 10027008 | tf_op jit(solution)/shard_map/all_gather | solution.py:64
  398.2 3.6 copy-start.3
  398.2 121.9 %copy-start.7 = (s32[4]{0:T(128)S(1)}, s32[4]{0:T(128)}, u32[]{:S(2)}) copy-start(s32[4]{0:T(128)} %param.18) | copy-start | bytes 52
  400.6 260.4 %all-reduce.3.cloned.1.call-start = ((), (), s32[]{:S(2)}) async-start(), calls=%async_computation.2 | async-start | bytes 1572864 | tf_op jit(solution)/shard_map/psum | solution.py:95
  619.4 16.7 %slice-start.2 = ((s8[4718592]{0:T(1024)(128)(4,1)}), s8[524288]{0:T(1024)(128)(4,1)S(1)}, s32[]{:S(2)}) async-start(s8[4718592]{0:T(1024)(128)(4,1)} %bitcast.66), calls=%async_computation.5 | async-start | bytes 1048576
  627.6 8.5 %slice-start.3 = ((s8[4718592]{0:T(1024)(128)(4,1)}), s8[4194304]{0:T(1024)(128)(4,1)S(1)}, s32[]{:S(2)}) async-start(s8[4718592]{0:T(1024)(128)(4,1)} %bitcast.66), calls=%async_computation.6 | async-start | bytes 8388608
  635.2 6.5 slice-start
  636.1 5.7 slice-start.1
  641.8 1.9 copy-start.8
  641.8 19.2 %copy-start.1 = (bf16[4,32,1536]{2,1,0:T(8,128)(2,1)S(1)}, bf16[4,32,1536]{2,1,0:T(8,128)(2,1)}, u32[]{:S(2)}) copy-start(bf16[4,32,1536]{2,1,0:T(8,128)(2,1)} %param.10) | copy-start | bytes 1179652
  641.8 19.2 %copy-start.2 = (f32[4,32,1536]{2,1,0:T(8,128)S(1)}, f32[4,32,1536]{2,1,0:T(8,128)}, u32[]{:S(2)}) copy-start(f32[4,32,1536]{2,1,0:T(8,128)} %param.13) | copy-start | bytes 2359300
Sparse Core Ops, SparseCore 0:
  400.7 199.9 all-gather.1
  643.8 17.1 all-reduce.2
